TPU v7x, 256 devices: a 8x8x2 block of a 8x8x16 slice. The times are simulated.
256 devices in a mesh: group: 2 (over z), grid: 64 (over y, x), var: 2 (over core).
Axes of the slice: x: 8, y: 8, z: 2, core: 2. Of those that a mesh axis runs over, the one named last changes fastest.
The devices are a block of a 8x8x16 slice.
Arguments:
- tokens: bfloat16 [96, 768, 3, 512], P('group', 'grid'), parts along dimension 0, may hold values from -6 to 6
- key_mask: int32 [96, 768], P('group', 'grid'), parts along dimension 0, may hold values 0 or 1
- w_qkv: bfloat16 [3, 512, 512], P(None, None, 'var'), may hold values from -16 to 16
- w_proj: bfloat16 [512, 512], P('var'), may hold values from -0.25 to 0.25
- w_up: bfloat16 [512, 2048], P(None, 'var'), may hold values from -0.25 to 0.25
- w_down: bfloat16 [2048, 512], P('var'), may hold values from -0.125 to 0.125
- level_query: bfloat16 [13, 512], replicated, may hold values from -1200 to 1200
- w_dec_q: bfloat16 [512, 512], P(None, 'var'), may hold values from -0.25 to 0.25
- w_dec_kv: bfloat16 [2, 512, 512], P(None, None, 'var'), may hold values from -0.25 to 0.25
- w_dec_o: bfloat16 [512, 512], P('var'), may hold values from -0.25 to 0.25
- decode_matrix: float32 [512, 64], replicated, may hold values from -0.25 to 0.25
Outputs:
- estimated_maps: float32 [4, 26, 192, 3072], P('var', 'group', 'grid'), parts along dimension 1
There are 2 independent parts, one for each index of `group`. A program takes and returns all parts, laid end to end along the dimension named above; an argument that names none is the same for every part. Nothing has to cross between parts.
All inputs are finite; a program needn't handle non-finite values. No bound on the sum of `key_mask` on one device may be relied on, other than what follows from the above.
Results may differ from a plain program's by a relative error of at most 0.025.
Values may be sent and summed in bfloat16 or wider, within the bound.
A program may use at most 128 MiB of HBM per device.

v0:
```python
import functools

import jax
import jax.numpy as jnp
import numpy as np
from jax import lax
from jax.experimental import pallas as pl
from jax.experimental.pallas import tpu as pltpu
from jax.sharding import PartitionSpec as P

HD = 64
WIN = 6
LEV = 3
PIX = 4
NLEV = 13
HALF = 112
TOK = 2 * HALF
EPSILON = 1e-05
LOG2E = 1.4426950408889634
NEG = -1e30
BF = jnp.bfloat16
F32 = jnp.float32


def sizes(grid):
    dests = grid // 8
    band = WIN * PIX // dests
    rows = -(-(band * 12) // 8) * 8
    return dests, band, rows


def token_fields():
    t = np.arange(TOK)
    half, q = t // HALF, t % HALF
    valid = q < 108
    cj, r = q // 6, q % 6
    return half, cj // 3, cj % 3, r, valid


def main_tables(grid):
    dests, band, rows = sizes(grid)
    pick = np.zeros((192, 256), np.float32)
    pick2 = np.zeros((64, 64), np.float32)
    for w in range(4):
        for r in range(6):
            for cj in range(8):
                pick[w * 48 + cj * 6 + r, cj * 32 + 3 + 6 * w + r] = 1
            for cj in range(2):
                pick2[w * 16 + cj * 6 + r, cj * 32 + 3 + 6 * w + r] = 1
    half, c6, j, r, valid = token_fields()
    level_rows = np.zeros((384, TOK), np.float32)
    t = np.arange(TOK)[valid]
    patch = half * 36 + c6 * 6 + r
    level_rows[j[valid] * 128 + patch[valid], t] = 1
    out_rows = np.zeros((4, dests * rows, 128), np.float32)
    for d in range(dests):
        for slot in range(band):
            rr, a = divmod(band * d + slot, 4)
            for c in range(12):
                out_rows[a, d * rows + slot * 12 + c, (c // 6) * 36 + (c % 6) * 6 + rr] = 1
    mask_rows = np.zeros((8, 48, TOK), np.float32)
    for window in range(8):
        mask_rows[window, ((6 * window + 3 + r) % 48)[valid], t] = 1
    mask_cols = np.zeros((32, TOK), np.float32)
    mask_cols[np.where(half == 0, 6 + c6, 16 + c6)[valid], t] = 1
    seam = np.where((r >= 3)[:, None] == (r >= 3)[None, :], 0, NEG).astype(np.float32)
    order = np.zeros((64, 64), np.float32)
    for a in range(4):
        for vh in range(2):
            for b in range(4):
                for v in range(2):
                    order[((a * 2 + vh) * 4 + b) * 2 + v, ((vh * 2 + v) * 4 + a) * 4 + b] = 1
    return (
        jnp.asarray(pick, BF),
        jnp.asarray(pick2, BF),
        jnp.asarray(level_rows, BF),
        jnp.asarray(out_rows, BF),
        jnp.asarray(mask_rows, BF),
        jnp.asarray(mask_cols, F32),
        jnp.asarray(seam, F32),
        jnp.asarray(order, BF),
    )


def dot(a, b):
    return lax.dot_general(a, b, (((1,), (0,)), ((), ())), preferred_element_type=F32)


def dot_t(a, b):
    return lax.dot_general(a, b, (((1,), (1,)), ((), ())), preferred_element_type=F32)


def norm(values):
    center = values - jnp.mean(values, axis=-1, keepdims=True)
    spread = jnp.mean(center * center, axis=-1, keepdims=True)
    return (center * lax.rsqrt(spread + EPSILON)).astype(BF)


def split3(values):
    hi = values.astype(BF)
    rest = values - hi.astype(F32)
    mid = rest.astype(BF)
    return hi, mid, (rest - mid.astype(F32)).astype(BF)


def main_kernel(
    grid,
    tokens, mask, w_qkv, w_proj, w_up, w_down, query, w_dec_q, w_dec_kv, w_dec_o, decode_t,
    c_pick, c_pick2, c_level, c_out, c_mrow, c_mcol, c_seam, c_order,
    recv,
    tok, own, hsend, hrecv, b_qkv, b_proj, b_up, b_down, b_kt, b_gt, b_dq, qbd,
    v_query, v_dq, v_dkv, v_do, v_dec, pick, pick2, level, outm, mrow, mcol, seam, order,
    mask_own, mask_right, marks, hidden, diff, dwt, zpix, msg,
    lsem, wsend, wrecv, hssem, hrsem, osend, orecv,
):
    dests, band, rows = sizes(grid)
    me = lax.axis_index("grid")
    v = lax.axis_index("var")
    partner = {"var": 1 - v}
    west = {"grid": lax.rem(me + grid - 1, grid)}

    barrier = pltpu.get_barrier_semaphore()
    flat = me * 2 + v

    def greet(k, _):
        other = lax.rem(flat + k, 2 * grid)
        pl.semaphore_signal(
            barrier, inc=1, device_id={"grid": other // 2, "var": lax.rem(other, 2)}, device_id_type=pl.DeviceIdType.MESH
        )
        return 0

    lax.fori_loop(1, 2 * grid, greet, 0)

    row0 = pl.multiple_of(24 * v, 8)
    row1 = pl.multiple_of(lax.rem(24 * v + 24, 48), 8)
    loads = [
        (tokens.at[:, pl.ds(row0, 24), :], tok.at[:, pl.ds(0, 24), :]),
        (tokens.at[:, pl.ds(row1, 8), :], tok.at[:, pl.ds(24, 8), :]),
        (c_pick, pick),
        (c_pick2, pick2),
        (w_dec_o, v_do),
        (decode_t, v_dec),
        (c_order, order),
        (w_dec_kv, v_dkv),
        (query, v_query),
        (w_dec_q, v_dq),
        (mask, mask_own),
        (w_qkv, b_qkv.at[v]),
        (c_mrow, mrow),
        (c_mcol, mcol),
        (c_seam, seam),
        (w_proj, b_proj.at[v]),
        (w_up, b_up.at[v]),
        (w_down, b_down.at[v]),
        (c_level, level),
        (c_out, outm),
    ]
    local = [pltpu.make_async_copy(src, dst, lsem.at[i]) for i, (src, dst) in enumerate(loads)]
    for copy in local:
        copy.start()

    for i in range(4):
        local[i].wait()
    for part, target in ((0, hsend), (18, own)):
        for block in range(2):
            src = tok[part + 8 * block : part + 8 * block + 8].reshape(256, 512)
            packed = dot(pick[...], src).astype(BF)
            for w in range(4):
                target[w, 48 * block : 48 * block + 48, :] = packed[48 * w : 48 * w + 48]
        src = tok[part + 16 : part + 18].reshape(64, 512)
        packed = dot(pick2[...], src).astype(BF)
        for w in range(4):
            target[w, 96:112, :] = packed[16 * w : 16 * w + 16]

    for i in range(4, 10):
        local[i].wait()
    dec = v_dec[...]
    hi, mid, low = split3(dec)
    do = v_do[...]
    unembed = (dot_t(hi, do) + dot_t(mid, do) + dot_t(low, do)).astype(BF)
    unembed = dot(order[...], unembed).astype(BF)
    lane = lax.broadcasted_iota(jnp.int32, (64, 256), 1)
    for h in range(4):
        block = jnp.where((lane >= 64 * h) & (lane < 64 * h + 64), unembed.astype(F32), 0).astype(BF)
        b_gt[v, 64 * h : 64 * h + 64, :] = dot_t(block, v_dkv[1]).astype(BF)
    eye = jnp.where(
        lax.broadcasted_iota(jnp.int32, (256, 256), 0) == lax.broadcasted_iota(jnp.int32, (256, 256), 1), 1.0, 0.0
    ).astype(BF)
    b_kt[v] = dot_t(eye, v_dkv[0]).astype(BF)
    b_dq[v, 0:13, :] = dot(v_query[...], v_dq[...])
    b_dq[v, 13:16, :] = jnp.zeros((3, 256), F32)

    pl.semaphore_wait(barrier, 2 * grid - 1)

    def remote(src, dst, send, recv_sem, where):
        return pltpu.make_async_remote_copy(
            src_ref=src, dst_ref=dst, send_sem=send, recv_sem=recv_sem, device_id=where, device_id_type=pl.DeviceIdType.MESH
        )

    def halo(w):
        return remote(hsend.at[w], hrecv.at[w], hssem.at[w], hrsem.at[w], west)

    mask_copy = remote(mask, mask_right, hssem.at[4], hrsem.at[4], west)
    mask_copy.start()
    for step in range(4):
        halo(lax.rem(me + 3 + step, 4)).start()
    weights = [
        (w_qkv, b_qkv.at[v]),
        (w_proj, b_proj.at[v]),
        (w_up, b_up.at[v]),
        (w_down, b_down.at[v]),
        (b_kt.at[v], b_kt.at[v]),
        (b_gt.at[v], b_gt.at[v]),
        (b_dq.at[v], b_dq.at[v]),
    ]
    shared = [remote(src, dst, wsend.at[i], wrecv.at[i], partner) for i, (src, dst) in enumerate(weights)]
    for copy in shared:
        copy.start()
    zpix[...] = jnp.zeros_like(zpix)
    marks[...] = jnp.zeros_like(marks)

    for i in range(10, len(local)):
        local[i].wait()
    mask_copy.wait()
    marks[0:12, :] = mask_own[...].astype(F32)
    marks[16:28, :] = mask_right[...].astype(F32)
    for copy in shared:
        copy.wait()
    lane2 = lax.broadcasted_iota(jnp.int32, (16, 256), 1)
    for g in range(2):
        dq = b_dq[g] * (HD ** -0.5)
        for h in range(4):
            part = jnp.where((lane2 >= 64 * h) & (lane2 < 64 * h + 64), dq, 0.0)
            hi = part.astype(BF)
            qbd[g, 16 * h : 16 * h + 16, :] = hi
            qbd[g, 64 + 16 * h : 80 + 16 * h, :] = (part - hi.astype(F32)).astype(BF)

    pair_lane = lax.broadcasted_iota(jnp.int32, (TOK, 128), 1)
    ones = jnp.ones((TOK, 128), BF)

    def window(step, _):
        w = lax.rem(me + step, 4)
        halo(w).wait_recv()
        x = jnp.concatenate([own[w], hrecv[w]], axis=0).astype(F32)
        n1 = norm(x)
        kept = jnp.sum(dot(marks[...].astype(BF), mrow[4 * v + w]) * mcol[...], axis=0, keepdims=True)
        last = jnp.where(4 * v + w == 7, 1.0, 0.0)
        bias = seam[...] * last + jnp.where(kept > 0.5, 0.0, NEG)
        diagonal = lax.broadcasted_iota(jnp.int32, (TOK, TOK), 0) == lax.broadcasted_iota(jnp.int32, (TOK, TOK), 1)
        bias = jnp.where(diagonal, 0.0, bias)
        attended = jnp.zeros((TOK, 512), F32)
        for g in range(2):
            q = (dot(n1, b_qkv[g, 0]).astype(BF)) * BF(HD ** -0.5)
            k = dot(n1, b_qkv[g, 1]).astype(BF)
            val = dot(n1, b_qkv[g, 2]).astype(BF)
            contexts = []
            for pair in range(2):
                cut = slice(128 * pair, 128 * pair + 128)
                context = None
                for side in range(2):
                    inside = (pair_lane >= 64 * side) & (pair_lane < 64 * side + 64)
                    qs = jnp.where(inside, q[:, cut], BF(0))
                    vs = jnp.where(inside, val[:, cut], BF(0))
                    scores = dot_t(qs, k[:, cut]) + bias
                    top = jnp.max(scores, axis=-1, keepdims=True)
                    probs = jnp.exp2((scores - top) * LOG2E).astype(BF)
                    both = dot(probs, jnp.concatenate([vs, ones], axis=1))
                    part = both[:, :128] * (1.0 / both[:, 128:])
                    context = part if context is None else context + part
                contexts.append(context.astype(BF))
            attended = attended + dot(jnp.concatenate(contexts, axis=1), b_proj[g])
        x1 = x + attended
        n2 = norm(x1)
        for g in range(2):
            for c in range(2):
                h = dot(n2, b_up[g, :, 512 * c : 512 * c + 512])
                h = 0.5 * h * (1.0 + lax.erf(h * (2.0 ** -0.5)))
                hidden[:, 1024 * g + 512 * c : 1024 * g + 512 * c + 512] = h.astype(BF)
        grown = x1 + dot(hidden[:, :1024], b_down[0]) + dot(hidden[:, 1024:], b_down[1])
        n3 = norm(grown.astype(BF).astype(F32))
        by_level = dot(level[...], n3).astype(BF)
        base = jnp.zeros((64, 128), F32)
        for g in range(2):
            kt = dot_t(b_kt[g], by_level).astype(BF)
            both = dot(qbd[g], kt)
            scores = both[:64] + both[64:]
            s0, s1, s2 = scores[:, :128], scores[:, 128:256], scores[:, 256:]
            top = jnp.maximum(jnp.maximum(s0, s1), s2)
            e0, e1, e2 = (jnp.exp2((s - top) * LOG2E) for s in (s0, s1, s2))
            scale = 1.0 / (e0 + e1 + e2)
            dwt[g, 0] = e0 * scale
            dwt[g, 1] = e1 * scale
            vals = dot_t(b_gt[g], by_level)
            last_level = vals[:, 256:]
            d0, d1 = vals[:, :128] - last_level, vals[:, 128:256] - last_level
            for h in range(4):
                diff[g, h, 0] = d0[64 * h : 64 * h + 64]
                diff[g, h, 1] = d1[64 * h : 64 * h + 64]
                base = base + last_level[64 * h : 64 * h + 64]
        for l in range(NLEV):
            total = base
            for g in range(2):
                for h in range(4):
                    for j in range(2):
                        total = total + dwt[g, j, 16 * h + l : 16 * h + l + 1, :] * diff[g, h, j]
            zpix[pl.ds(l, 64, stride=16), :] = total
        packed = jnp.zeros((dests * rows, 256), F32)
        for a in range(4):
            packed = packed + dot_t(outm[a], zpix[256 * a : 256 * a + 256, :].astype(BF))
        for d in range(dests):
            for side in range(2):
                msg[w, side, d] = packed[rows * d : rows * d + rows, 128 * side : 128 * side + 128].astype(BF)
        for d in range(dests):
            to = lax.rem((4 * v + w) * dests + dests // 2 + d, grid)
            for side in range(2):
                mine = (to == me) & (v == side)

                @pl.when(mine)
                def _():
                    pltpu.make_async_copy(msg.at[w, side, d], recv.at[me], orecv).start()

                @pl.when(jnp.logical_not(mine))
                def _():
                    remote(msg.at[w, side, d], recv.at[me], osend, orecv, {"grid": to, "var": side}).start()

        return 0

    lax.fori_loop(0, 4, window, 0)
    for w in range(4):
        halo(w).wait_send()
    my_window = lax.rem(me + grid - dests // 2, grid) // dests
    stays = my_window // 4 == v
    pltpu.make_async_copy(recv, recv, orecv).wait()

    @pl.when(stays)
    def _():
        part = recv.at[pl.ds(0, grid - 1)]
        pltpu.make_async_copy(part, part, osend).wait()

    @pl.when(jnp.logical_not(stays))
    def _():
        pltpu.make_async_copy(recv, recv, osend).wait()


def final_tables(grid):
    _, band, _ = sizes(grid)
    pad = -(-26 * band // 16) * 16
    rows = np.zeros((band, 4 * pad, 128), np.float32)
    for slot in range(band):
        for b in range(4):
            for l in range(NLEV):
                for v in range(2):
                    rows[slot, b * pad + (l * band + slot) * 2 + v, (b * 2 + v) * 16 + l] = 1
    tile = np.gcd(12 * grid, 128)
    spread = np.zeros((4, tile, 4 * tile), np.float32)
    for b in range(4):
        spread[b, np.arange(tile), 4 * np.arange(tile) + b] = 1
    return jnp.asarray(rows, BF), jnp.asarray(spread.reshape(2, 2 * tile, 4 * tile), BF)


def final_kernel(grid, recv, sel, spread, out, stage):
    _, band, _ = sizes(grid)
    cells = 12 * grid
    pad = sel.shape[1] // 4
    for s in range(grid):
        block = recv[s].astype(F32)
        start = 12 * s + 6
        for slot in range(band):
            piece = block[12 * slot : 12 * slot + 12]
            if start + 12 <= cells:
                stage[slot, start : start + 12, :] = piece
            else:
                stage[slot, start : start + 6, :] = piece[:6]
                stage[slot, 0:6, :] = piece[6:]
    flipped = jnp.zeros((4 * pad, cells), F32)
    for slot in range(band):
        flipped = flipped + dot_t(sel[slot], stage[slot].astype(BF))
    flipped = flipped.astype(BF)
    tile = spread.shape[2] // 4
    tiles = cells // tile

    def stacked(b):
        return jnp.concatenate(
            [flipped[b * pad : b * pad + pad, tile * m : tile * m + tile] for m in range(tiles)], axis=0
        )

    lines = dot(jnp.concatenate([stacked(0), stacked(1)], axis=1), spread[0]) + dot(
        jnp.concatenate([stacked(2), stacked(3)], axis=1), spread[1]
    )
    for m in range(tiles):
        for k in range(NLEV * band):
            out[k, :, 4 * tile * m : 4 * tile * (m + 1)] = lines[m * pad + 2 * k : m * pad + 2 * k + 2]


def pixels_of(grid, tokens, key_mask, w_qkv, w_proj, w_up, w_down, level_query, w_dec_q, w_dec_kv, w_dec_o, decode_matrix):
    dests, band, rows = sizes(grid)
    by_column = jnp.transpose(tokens, (1, 2, 0, 3)).reshape(36, 48, 512)
    tables = main_tables(grid)
    operands = (
        by_column, key_mask.T, w_qkv, w_proj, w_up, w_down, level_query, w_dec_q, w_dec_kv, w_dec_o, decode_matrix.T,
    ) + tables
    vm = pltpu.VMEM
    return pl.pallas_call(
        functools.partial(main_kernel, grid),
        out_shape=jax.ShapeDtypeStruct((grid, rows, 128), BF),
        in_specs=[pl.BlockSpec(memory_space=pl.ANY)] * len(operands),
        out_specs=pl.BlockSpec(memory_space=pl.ANY),
        scratch_shapes=[
            vm((36, 32, 512), BF),
            vm((4, HALF, 512), BF),
            vm((4, HALF, 512), BF),
            vm((4, HALF, 512), BF),
            vm((2, 3, 512, 256), BF),
            vm((2, 256, 512), BF),
            vm((2, 512, 1024), BF),
            vm((2, 1024, 512), BF),
            vm((2, 256, 512), BF),
            vm((2, 256, 512), BF),
            vm((2, 16, 256), F32),
            vm((2, 128, 256), BF),
            vm((13, 512), BF),
            vm((512, 256), BF),
            vm((2, 512, 256), BF),
            vm((256, 512), BF),
            vm((64, 512), F32),
            *[vm(table.shape, table.dtype) for table in tables],
            vm((12, 48), jnp.int32),
            vm((12, 48), jnp.int32),
            vm((32, 48), F32),
            vm((TOK, 2048), BF),
            vm((2, 4, 2, 64, 128), F32),
            vm((2, 2, 64, 128), F32),
            vm((1024, 128), F32),
            vm((4, 2, dests, rows, 128), BF),
            pltpu.SemaphoreType.DMA((20,)),
            pltpu.SemaphoreType.DMA((7,)),
            pltpu.SemaphoreType.DMA((7,)),
            pltpu.SemaphoreType.DMA((5,)),
            pltpu.SemaphoreType.DMA((5,)),
            pltpu.SemaphoreType.DMA,
            pltpu.SemaphoreType.DMA,
        ],
        compiler_params=pltpu.CompilerParams(
            collective_id=0, has_side_effects=True, vmem_limit_bytes=60 * 2**20
        ),
    )(*operands)


def assemble(grid, received):
    _, band, _ = sizes(grid)
    tables = final_tables(grid)
    lines = pl.pallas_call(
        functools.partial(final_kernel, grid),
        out_shape=jax.ShapeDtypeStruct((NLEV * band, 2, 48 * grid), F32),
        scratch_shapes=[pltpu.VMEM((band, 12 * grid, 128), F32)],
        compiler_params=pltpu.CompilerParams(vmem_limit_bytes=60 * 2**20),
    )(received, *tables)
    return jnp.transpose(lines.reshape(NLEV, band, 2, 48 * grid), (2, 0, 1, 3))


def local(*args):
    grid = lax.axis_size("grid")
    return assemble(grid, pixels_of(grid, *args))


def solution(mesh):
    placed = (
        P("group", "grid", None, None),
        P("group", "grid"),
        P(None, None, "var"),
        P("var", None),
        P(None, "var"),
        P("var", None),
        P(),
        P(None, "var"),
        P(None, None, "var"),
        P("var", None),
        P(),
    )
    return jax.shard_map(
        local, mesh=mesh, in_specs=placed, out_specs=P("var", "group", "grid", None), check_vma=False
    )
```

profile of v0, /device:TPU:513, one launch (start us, length us, event | category | flops | bytes accessed | tf_op | source)
XLA Modules:
  0.0 68.8 jit_solution(173984699100529539)
XLA Ops:
  0.0 65.3 %shard_map.199.recv = bf16[64,40,128]{2,1,0:T(8,128)(2,1)} custom-call(bf16[36,48,512]{2,1,0:T(8,128)(2,1)} %bitcast.8, s32[12,48]{1,0:T(8,128)} %bitcast.10, bf16[3,512,256]{2,1,0:T(8,128)(2,1)} %w_qkv.1, bf16[256,512]{1,0:T(8,128)(2,1)} %w_proj.1, bf16[512,1024]{1,0:T(8,128)(2,1)} %w_up.1, bf16[1024,512]{1,0:T(8,128)(2,1)} %w_down.1, ...), custom_call_target="tpu_custom_call" | custom-call | tf_op jit(solution)/shard_map/pallas_call | solution.py:403
  65.3 3.4 %shard_map.200 = f32[39,2,3072]{2,1,0:T(2,128)} custom-call(bf16[64,40,128]{2,1,0:T(8,128)(2,1)} %shard_map.199.recv, bf16[3,320,128]{2,1,0:T(8,128)(2,1)} %constant.28.clone.sel, bf16[2,256,512]{2,1,0:T(8,128)(2,1)} %constant.29.clone.spread), custom_call_target="tpu_custom_call" | custom-call | tf_op jit(solution)/shard_map/pallas_call | solution.py:452
where the time goes:
time: 68.9 us; the launch traced here: 68.8 us
  Pallas kernels  68.8 us (100%)
    pallas_call x1, Pallas kernels, pixels_of(): pl.pallas_call(functools.partial(main_kernel, grid), out_shape=jax.ShapeD...  65.3 us
    pallas_call x1, Pallas kernels, assemble(): pl.pallas_call(functools.partial(final_kernel, grid), out_shape=jax.Shape...  3.44 us

commit v1 on v0

--- a/solution.py
+++ b/solution.py
@@ -22,11 +22,29 @@
 F32 = jnp.float32
 
 
+SLOTS = 4
+
+
+def window_of(v, slot):
+    return (7 * v + 2 * slot) % 8
+
+
 def sizes(grid):
     dests = grid // 8
     band = WIN * PIX // dests
     rows = -(-(band * 12) // 8) * 8
     return dests, band, rows
+
+
+def reach(grid):
+    stride = int(round(grid**0.5)) if grid > 8 else 2
+    radius = 0
+    for k in range(grid):
+        ways = [abs(b) + min((k - stride * b) % grid, (stride * b - k) % grid) for b in range(-stride, stride + 1)]
+        radius = max(radius, min(ways))
+    rounds = max(0, (radius - 1).bit_length())
+    assert rounds <= 3
+    return stride, rounds
 
 
 def token_fields():
@@ -39,14 +57,16 @@
 
 def main_tables(grid):
     dests, band, rows = sizes(grid)
-    pick = np.zeros((192, 256), np.float32)
-    pick2 = np.zeros((64, 64), np.float32)
-    for w in range(4):
-        for r in range(6):
-            for cj in range(8):
-                pick[w * 48 + cj * 6 + r, cj * 32 + 3 + 6 * w + r] = 1
-            for cj in range(2):
-                pick2[w * 16 + cj * 6 + r, cj * 32 + 3 + 6 * w + r] = 1
+    pick = np.zeros((2, SLOTS * 48, 8 * 48), np.float32)
+    pick2 = np.zeros((2, SLOTS * 16, 2 * 48), np.float32)
+    for v in range(2):
+        for step in range(SLOTS):
+            for r in range(6):
+                row = (6 * int(window_of(v, step)) + 3 + r) % 48
+                for cj in range(8):
+                    pick[v, step * 48 + cj * 6 + r, cj * 48 + row] = 1
+                for cj in range(2):
+                    pick2[v, step * 16 + cj * 6 + r, cj * 48 + row] = 1
     half, c6, j, r, valid = token_fields()
     level_rows = np.zeros((384, TOK), np.float32)
     t = np.arange(TOK)[valid]
@@ -108,10 +128,10 @@
     tokens, mask, w_qkv, w_proj, w_up, w_down, query, w_dec_q, w_dec_kv, w_dec_o, decode_t,
     c_pick, c_pick2, c_level, c_out, c_mrow, c_mcol, c_seam, c_order,
     recv,
-    tok, own, hsend, hrecv, b_qkv, b_proj, b_up, b_down, b_kt, b_gt, b_dq, qbd,
+    tok, own, hsend, hrecv, xone, b_qkv, b_proj, b_up, b_down, b_kg, b_dq, qbd,
     v_query, v_dq, v_dkv, v_do, v_dec, pick, pick2, level, outm, mrow, mcol, seam, order,
     mask_own, mask_right, marks, hidden, diff, dwt, zpix, msg,
-    lsem, wsend, wrecv, hssem, hrsem, osend, orecv,
+    lsem, wsend, wrecv, hssem, hrsem, osend, orecv, heard,
 ):
     dests, band, rows = sizes(grid)
     me = lax.axis_index("grid")
@@ -120,24 +140,32 @@
     west = {"grid": lax.rem(me + grid - 1, grid)}
 
     barrier = pltpu.get_barrier_semaphore()
-    flat = me * 2 + v
-
-    def greet(k, _):
-        other = lax.rem(flat + k, 2 * grid)
-        pl.semaphore_signal(
-            barrier, inc=1, device_id={"grid": other // 2, "var": lax.rem(other, 2)}, device_id_type=pl.DeviceIdType.MESH
-        )
-        return 0
-
-    lax.fori_loop(1, 2 * grid, greet, 0)
-
-    row0 = pl.multiple_of(24 * v, 8)
-    row1 = pl.multiple_of(lax.rem(24 * v + 24, 48), 8)
+
+    def signal(sem, where):
+        pl.semaphore_signal(sem, inc=1, device_id=where, device_id_type=pl.DeviceIdType.MESH)
+
+    stride, rounds = reach(grid)
+    sides = (1, grid - 1, stride, grid - stride)
+    signal(barrier, partner)
+    for by in sides:
+        signal(barrier, {"grid": lax.rem(me + by, grid)})
+
+    def tell(k):
+        if k < rounds:
+            for by in sides:
+                signal(heard.at[k], {"grid": lax.rem(me + by * 2**k, grid)})
+        elif k == rounds:
+            signal(heard.at[k], partner)
+
+    def hear(k):
+        if k <= rounds:
+            pl.semaphore_wait(heard.at[k], 4 if k < rounds else 1)
+
     loads = [
-        (tokens.at[:, pl.ds(row0, 24), :], tok.at[:, pl.ds(0, 24), :]),
-        (tokens.at[:, pl.ds(row1, 8), :], tok.at[:, pl.ds(24, 8), :]),
-        (c_pick, pick),
-        (c_pick2, pick2),
+        (tokens.at[pl.ds(0, 18)], tok.at[pl.ds(0, 18)]),
+        (c_pick.at[v], pick),
+        (c_pick2.at[v], pick2),
+        (tokens.at[pl.ds(18, 18)], tok.at[pl.ds(18, 18)]),
         (w_dec_o, v_do),
         (decode_t, v_dec),
         (c_order, order),
@@ -159,18 +187,50 @@
     for copy in local:
         copy.start()
 
-    for i in range(4):
+    def remote(src, dst, send, recv_sem, where):
+        return pltpu.make_async_remote_copy(
+            src_ref=src, dst_ref=dst, send_sem=send, recv_sem=recv_sem, device_id=where, device_id_type=pl.DeviceIdType.MESH
+        )
+
+    def halo(w):
+        return remote(hsend.at[w], hrecv.at[w], hssem.at[w], hrsem.at[w], west)
+
+    weights = [
+        (w_qkv, b_qkv.at[v]),
+        (w_proj, b_proj.at[v]),
+        (w_up, b_up.at[v]),
+        (w_down, b_down.at[v]),
+        (b_kg.at[v], b_kg.at[v]),
+        (b_kg.at[2 + v], b_kg.at[2 + v]),
+        (b_dq.at[v], b_dq.at[v]),
+    ]
+    shared = [remote(src, dst, wsend.at[i], wrecv.at[i], partner) for i, (src, dst) in enumerate(weights)]
+    mask_copy = remote(mask, mask_right, hssem.at[SLOTS], hrsem.at[SLOTS], west)
+
+    def pack(part, target):
+        for block in range(2):
+            src = tok[part + 8 * block : part + 8 * block + 8].reshape(384, 512)
+            packed = dot(pick[...], src).astype(BF)
+            for w in range(SLOTS):
+                target[w, 48 * block : 48 * block + 48, :] = packed[48 * w : 48 * w + 48]
+        src = tok[part + 16 : part + 18].reshape(96, 512)
+        packed = dot(pick2[...], src).astype(BF)
+        for w in range(SLOTS):
+            target[w, 96:112, :] = packed[16 * w : 16 * w + 16]
+
+    pl.semaphore_wait(barrier, 5)
+    for copy in shared[:4]:
+        copy.start()
+    mask_copy.start()
+    tell(0)
+
+    for i in range(3):
         local[i].wait()
-    for part, target in ((0, hsend), (18, own)):
-        for block in range(2):
-            src = tok[part + 8 * block : part + 8 * block + 8].reshape(256, 512)
-            packed = dot(pick[...], src).astype(BF)
-            for w in range(4):
-                target[w, 48 * block : 48 * block + 48, :] = packed[48 * w : 48 * w + 48]
-        src = tok[part + 16 : part + 18].reshape(64, 512)
-        packed = dot(pick2[...], src).astype(BF)
-        for w in range(4):
-            target[w, 96:112, :] = packed[16 * w : 16 * w + 16]
+    pack(0, hsend)
+    for step in range(SLOTS):
+        halo(lax.rem(me + grid - 1 + step, SLOTS)).start()
+    local[3].wait()
+    pack(18, own)
 
     for i in range(4, 10):
         local[i].wait()
@@ -182,40 +242,18 @@
     lane = lax.broadcasted_iota(jnp.int32, (64, 256), 1)
     for h in range(4):
         block = jnp.where((lane >= 64 * h) & (lane < 64 * h + 64), unembed.astype(F32), 0).astype(BF)
-        b_gt[v, 64 * h : 64 * h + 64, :] = dot_t(block, v_dkv[1]).astype(BF)
+        b_kg[2 + v, 64 * h : 64 * h + 64, :] = dot_t(block, v_dkv[1]).astype(BF)
     eye = jnp.where(
         lax.broadcasted_iota(jnp.int32, (256, 256), 0) == lax.broadcasted_iota(jnp.int32, (256, 256), 1), 1.0, 0.0
     ).astype(BF)
-    b_kt[v] = dot_t(eye, v_dkv[0]).astype(BF)
+    b_kg[v] = dot_t(eye, v_dkv[0]).astype(BF)
     b_dq[v, 0:13, :] = dot(v_query[...], v_dq[...])
     b_dq[v, 13:16, :] = jnp.zeros((3, 256), F32)
 
-    pl.semaphore_wait(barrier, 2 * grid - 1)
-
-    def remote(src, dst, send, recv_sem, where):
-        return pltpu.make_async_remote_copy(
-            src_ref=src, dst_ref=dst, send_sem=send, recv_sem=recv_sem, device_id=where, device_id_type=pl.DeviceIdType.MESH
-        )
-
-    def halo(w):
-        return remote(hsend.at[w], hrecv.at[w], hssem.at[w], hrsem.at[w], west)
-
-    mask_copy = remote(mask, mask_right, hssem.at[4], hrsem.at[4], west)
-    mask_copy.start()
-    for step in range(4):
-        halo(lax.rem(me + 3 + step, 4)).start()
-    weights = [
-        (w_qkv, b_qkv.at[v]),
-        (w_proj, b_proj.at[v]),
-        (w_up, b_up.at[v]),
-        (w_down, b_down.at[v]),
-        (b_kt.at[v], b_kt.at[v]),
-        (b_gt.at[v], b_gt.at[v]),
-        (b_dq.at[v], b_dq.at[v]),
-    ]
-    shared = [remote(src, dst, wsend.at[i], wrecv.at[i], partner) for i, (src, dst) in enumerate(weights)]
-    for copy in shared:
+    for copy in shared[4:]:
         copy.start()
+    hear(0)
+    tell(1)
     zpix[...] = jnp.zeros_like(zpix)
     marks[...] = jnp.zeros_like(marks)
 
@@ -224,36 +262,25 @@
     mask_copy.wait()
     marks[0:12, :] = mask_own[...].astype(F32)
     marks[16:28, :] = mask_right[...].astype(F32)
-    for copy in shared:
-        copy.wait()
-    lane2 = lax.broadcasted_iota(jnp.int32, (16, 256), 1)
-    for g in range(2):
-        dq = b_dq[g] * (HD ** -0.5)
-        for h in range(4):
-            part = jnp.where((lane2 >= 64 * h) & (lane2 < 64 * h + 64), dq, 0.0)
-            hi = part.astype(BF)
-            qbd[g, 16 * h : 16 * h + 16, :] = hi
-            qbd[g, 64 + 16 * h : 80 + 16 * h, :] = (part - hi.astype(F32)).astype(BF)
-
     pair_lane = lax.broadcasted_iota(jnp.int32, (TOK, 128), 1)
     ones = jnp.ones((TOK, 128), BF)
 
-    def window(step, _):
-        w = lax.rem(me + step, 4)
-        halo(w).wait_recv()
+    def attend(w):
+        which = window_of(v, w)
         x = jnp.concatenate([own[w], hrecv[w]], axis=0).astype(F32)
         n1 = norm(x)
-        kept = jnp.sum(dot(marks[...].astype(BF), mrow[4 * v + w]) * mcol[...], axis=0, keepdims=True)
-        last = jnp.where(4 * v + w == 7, 1.0, 0.0)
+        kept = jnp.sum(dot(marks[...].astype(BF), mrow[which]) * mcol[...], axis=0, keepdims=True)
+        last = jnp.where(which == 7, 1.0, 0.0)
         bias = seam[...] * last + jnp.where(kept > 0.5, 0.0, NEG)
         diagonal = lax.broadcasted_iota(jnp.int32, (TOK, TOK), 0) == lax.broadcasted_iota(jnp.int32, (TOK, TOK), 1)
         bias = jnp.where(diagonal, 0.0, bias)
-        attended = jnp.zeros((TOK, 512), F32)
+        yield
+        contexts = []
         for g in range(2):
             q = (dot(n1, b_qkv[g, 0]).astype(BF)) * BF(HD ** -0.5)
             k = dot(n1, b_qkv[g, 1]).astype(BF)
             val = dot(n1, b_qkv[g, 2]).astype(BF)
-            contexts = []
+            yield
             for pair in range(2):
                 cut = slice(128 * pair, 128 * pair + 128)
                 context = None
@@ -267,21 +294,32 @@
                     both = dot(probs, jnp.concatenate([vs, ones], axis=1))
                     part = both[:, :128] * (1.0 / both[:, 128:])
                     context = part if context is None else context + part
+                    yield
                 contexts.append(context.astype(BF))
-            attended = attended + dot(jnp.concatenate(contexts, axis=1), b_proj[g])
-        x1 = x + attended
+        attended = dot(jnp.concatenate(contexts[:2], axis=1), b_proj[0])
+        xone[w] = x + attended + dot(jnp.concatenate(contexts[2:], axis=1), b_proj[1])
+        yield
+
+    def finish(w):
+        x1 = xone[w]
         n2 = norm(x1)
+        yield
         for g in range(2):
             for c in range(2):
                 h = dot(n2, b_up[g, :, 512 * c : 512 * c + 512])
                 h = 0.5 * h * (1.0 + lax.erf(h * (2.0 ** -0.5)))
                 hidden[:, 1024 * g + 512 * c : 1024 * g + 512 * c + 512] = h.astype(BF)
+                yield
         grown = x1 + dot(hidden[:, :1024], b_down[0]) + dot(hidden[:, 1024:], b_down[1])
+        yield
         n3 = norm(grown.astype(BF).astype(F32))
+        yield
         by_level = dot(level[...], n3).astype(BF)
         base = jnp.zeros((64, 128), F32)
+        all_kg = dot_t(b_kg[...].reshape(1024, 512), by_level)
+        yield
         for g in range(2):
-            kt = dot_t(b_kt[g], by_level).astype(BF)
+            kt = all_kg[256 * g : 256 * g + 256].astype(BF)
             both = dot(qbd[g], kt)
             scores = both[:64] + both[64:]
             s0, s1, s2 = scores[:, :128], scores[:, 128:256], scores[:, 256:]
@@ -290,13 +328,14 @@
             scale = 1.0 / (e0 + e1 + e2)
             dwt[g, 0] = e0 * scale
             dwt[g, 1] = e1 * scale
-            vals = dot_t(b_gt[g], by_level)
+            vals = all_kg[512 + 256 * g : 768 + 256 * g]
             last_level = vals[:, 256:]
             d0, d1 = vals[:, :128] - last_level, vals[:, 128:256] - last_level
             for h in range(4):
                 diff[g, h, 0] = d0[64 * h : 64 * h + 64]
                 diff[g, h, 1] = d1[64 * h : 64 * h + 64]
                 base = base + last_level[64 * h : 64 * h + 64]
+        yield
         for l in range(NLEV):
             total = base
             for g in range(2):
@@ -304,14 +343,24 @@
                     for j in range(2):
                         total = total + dwt[g, j, 16 * h + l : 16 * h + l + 1, :] * diff[g, h, j]
             zpix[pl.ds(l, 64, stride=16), :] = total
+            if l % 4 == 3:
+                yield
         packed = jnp.zeros((dests * rows, 256), F32)
         for a in range(4):
             packed = packed + dot_t(outm[a], zpix[256 * a : 256 * a + 256, :].astype(BF))
         for d in range(dests):
             for side in range(2):
                 msg[w, side, d] = packed[rows * d : rows * d + rows, 128 * side : 128 * side + 128].astype(BF)
+        yield
+
+    def run(*parts):
+        parts = list(parts)
+        while parts:
+            parts = [part for part in parts if next(part, 0) is None]
+
+    def send(w):
         for d in range(dests):
-            to = lax.rem((4 * v + w) * dests + dests // 2 + d, grid)
+            to = lax.rem(window_of(v, w) * dests + dests // 2 + d, grid)
             for side in range(2):
                 mine = (to == me) & (v == side)
 
@@ -321,25 +370,66 @@
 
                 @pl.when(jnp.logical_not(mine))
                 def _():
-                    remote(msg.at[w, side, d], recv.at[me], osend, orecv, {"grid": to, "var": side}).start()
-
+                    remote(msg.at[w, side, d], recv.at[me], osend.at[w], orecv, {"grid": to, "var": side}).start()
+
+    first = lax.rem(me, SLOTS)
+    halo(first).wait_recv()
+    hear(1)
+    tell(2)
+    shared[0].wait()
+    shared[1].wait()
+    run(attend(first))
+    hear(2)
+    tell(3)
+    for copy in shared[2:]:
+        copy.wait()
+    lane2 = lax.broadcasted_iota(jnp.int32, (16, 256), 1)
+    for g in range(2):
+        dq = b_dq[g] * (HD ** -0.5)
+        for h in range(4):
+            part = jnp.where((lane2 >= 64 * h) & (lane2 < 64 * h + 64), dq, 0.0)
+            hi = part.astype(BF)
+            qbd[g, 16 * h : 16 * h + 16, :] = hi
+            qbd[g, 64 + 16 * h : 80 + 16 * h, :] = (part - hi.astype(F32)).astype(BF)
+
+
+    def body(step, _):
+        now, later = lax.rem(me + step, SLOTS), lax.rem(me + step + 1, SLOTS)
+        halo(later).wait_recv()
+        run(finish(now), attend(later))
+
+        @pl.when(step == 0)
+        def _():
+            hear(3)
+
+        send(now)
         return 0
 
-    lax.fori_loop(0, 4, window, 0)
-    for w in range(4):
+    lax.fori_loop(0, SLOTS - 1, body, 0)
+    last = lax.rem(me + SLOTS - 1, SLOTS)
+    run(finish(last))
+    send(last)
+
+    my_window = lax.rem(me + grid - dests // 2, grid) // dests
+
+    def sent(w, _):
         halo(w).wait_send()
-    my_window = lax.rem(me + grid - dests // 2, grid) // dests
-    stays = my_window // 4 == v
+        stays = window_of(v, w) == my_window
+        row = recv.at[pl.ds(0, 2 * dests)]
+        most = recv.at[pl.ds(0, 2 * dests - 1)]
+
+        @pl.when(stays)
+        def _():
+            pltpu.make_async_copy(most, most, osend.at[w]).wait()
+
+        @pl.when(jnp.logical_not(stays))
+        def _():
+            pltpu.make_async_copy(row, row, osend.at[w]).wait()
+
+        return 0
+
+    lax.fori_loop(0, SLOTS, sent, 0)
     pltpu.make_async_copy(recv, recv, orecv).wait()
-
-    @pl.when(stays)
-    def _():
-        part = recv.at[pl.ds(0, grid - 1)]
-        pltpu.make_async_copy(part, part, osend).wait()
-
-    @pl.when(jnp.logical_not(stays))
-    def _():
-        pltpu.make_async_copy(recv, recv, osend).wait()
 
 
 def final_tables(grid):
@@ -403,19 +493,19 @@
     return pl.pallas_call(
         functools.partial(main_kernel, grid),
         out_shape=jax.ShapeDtypeStruct((grid, rows, 128), BF),
-        in_specs=[pl.BlockSpec(memory_space=pl.ANY)] * len(operands),
+        in_specs=[pl.BlockSpec(memory_space=pltpu.HBM)] * len(operands),
         out_specs=pl.BlockSpec(memory_space=pl.ANY),
         scratch_shapes=[
-            vm((36, 32, 512), BF),
-            vm((4, HALF, 512), BF),
-            vm((4, HALF, 512), BF),
-            vm((4, HALF, 512), BF),
+            vm((36, 48, 512), BF),
+            vm((SLOTS, HALF, 512), BF),
+            vm((SLOTS, HALF, 512), BF),
+            vm((SLOTS, HALF, 512), BF),
+            vm((SLOTS, TOK, 512), F32),
             vm((2, 3, 512, 256), BF),
             vm((2, 256, 512), BF),
             vm((2, 512, 1024), BF),
             vm((2, 1024, 512), BF),
-            vm((2, 256, 512), BF),
-            vm((2, 256, 512), BF),
+            vm((4, 256, 512), BF),
             vm((2, 16, 256), F32),
             vm((2, 128, 256), BF),
             vm((13, 512), BF),
@@ -423,7 +513,7 @@
             vm((2, 512, 256), BF),
             vm((256, 512), BF),
             vm((64, 512), F32),
-            *[vm(table.shape, table.dtype) for table in tables],
+            *[vm(table.shape[1:] if i < 2 else table.shape, table.dtype) for i, table in enumerate(tables)],
             vm((12, 48), jnp.int32),
             vm((12, 48), jnp.int32),
             vm((32, 48), F32),
@@ -431,14 +521,15 @@
             vm((2, 4, 2, 64, 128), F32),
             vm((2, 2, 64, 128), F32),
             vm((1024, 128), F32),
-            vm((4, 2, dests, rows, 128), BF),
+            vm((SLOTS, 2, dests, rows, 128), BF),
             pltpu.SemaphoreType.DMA((20,)),
             pltpu.SemaphoreType.DMA((7,)),
             pltpu.SemaphoreType.DMA((7,)),
-            pltpu.SemaphoreType.DMA((5,)),
-            pltpu.SemaphoreType.DMA((5,)),
+            pltpu.SemaphoreType.DMA((SLOTS + 1,)),
+            pltpu.SemaphoreType.DMA((SLOTS + 1,)),
+            pltpu.SemaphoreType.DMA((SLOTS,)),
             pltpu.SemaphoreType.DMA,
-            pltpu.SemaphoreType.DMA,
+            pltpu.SemaphoreType.REGULAR((4,)),
         ],
         compiler_params=pltpu.CompilerParams(
             collective_id=0, has_side_effects=True, vmem_limit_bytes=60 * 2**20
@@ -453,7 +544,7 @@
         functools.partial(final_kernel, grid),
         out_shape=jax.ShapeDtypeStruct((NLEV * band, 2, 48 * grid), F32),
         scratch_shapes=[pltpu.VMEM((band, 12 * grid, 128), F32)],
-        compiler_params=pltpu.CompilerParams(vmem_limit_bytes=60 * 2**20),
+        compiler_params=pltpu.CompilerParams(vmem_limit_bytes=32 * 2**20),
     )(received, *tables)
     return jnp.transpose(lines.reshape(NLEV, band, 2, 48 * grid), (2, 0, 1, 3))
 

time: 68.9 us -> 59.3 us (0.86)
  the two profiles are of different devices: /device:TPU:513 before, /device:TPU:529 now
where the time goes in v1:
time: 59.3 us; the launch traced here: 59.1 us
  Pallas kernels  58 us (98%)
  local copies, waits for them, and re-layouts  1.09 us (2%)
    pallas_call x1, Pallas kernels, pixels_of(): pl.pallas_call(functools.partial(main_kernel, grid), out_shape=jax.ShapeD...  55.9 us
    pallas_call x1, Pallas kernels, assemble(): pl.pallas_call(functools.partial(final_kernel, grid), out_shape=jax.Shape...  2.07 us

profile of v1, /device:TPU:529, one launch (start us, length us, event | category | flops | bytes accessed | tf_op | source)
XLA Modules:
  0.0 59.1 jit_solution(7037369511207165165)
XLA Ops:
  0.0 0.0 copy-start.1
  0.0 0.0 copy-start.2
  0.0 55.9 %shard_map.199.recv = bf16[64,40,128]{2,1,0:T(8,128)(2,1)} custom-call(bf16[36,48,512]{2,1,0:T(8,128)(2,1)} %bitcast.8, s32[12,48]{1,0:T(8,128)} %bitcast.10, bf16[3,512,256]{2,1,0:T(8,128)(2,1)} %w_qkv.1, bf16[256,512]{1,0:T(8,128)(2,1)} %w_proj.1, bf16[512,1024]{1,0:T(8,128)(2,1)} %w_up.1, bf16[1024,512]{1,0:T(8,128)(2,1)} %w_down.1, ...), custom_call_target="tpu_custom_call" | custom-call | tf_op jit(solution)/shard_map/pallas_call | solution.py:493
  55.9 0.0 copy-done.1
  56.0 0.0 copy-done.2
  56.0 0.0 copy-start
  56.0 1.1 %copy-done = bf16[64,40,128]{2,1,0:T(8,128)(2,1)S(1)} copy-done((bf16[64,40,128]{2,1,0:T(8,128)(2,1)S(1)}, bf16[64,40,128]{2,1,0:T(8,128)(2,1)}, u32[]{:S(2)}) %copy-start) | copy-done | bytes 655384
  57.1 2.1 %shard_map.200 = f32[39,2,3072]{2,1,0:T(2,128)} custom-call(bf16[64,40,128]{2,1,0:T(8,128)(2,1)S(1)} %copy-done, bf16[3,320,128]{2,1,0:T(8,128)(2,1)S(1)} %copy-done.2, bf16[2,256,512]{2,1,0:T(8,128)(2,1)S(1)} %copy-done.1), custom_call_target="tpu_custom_call" | custom-call | tf_op jit(solution)/shard_map/pallas_call | solution.py:543
Async XLA Ops:
  0.0 55.9 %copy-start.1 = (bf16[2,256,512]{2,1,0:T(8,128)(2,1)S(1)}, bf16[2,256,512]{2,1,0:T(8,128)(2,1)}, u32[]{:S(2)}) copy-start(bf16[2,256,512]{2,1,0:T(8,128)(2,1)} %constant.29.clone.spread) | copy-start | bytes 1572868
  0.0 56.0 %copy-start.2 = (bf16[3,320,128]{2,1,0:T(8,128)(2,1)S(1)}, bf16[3,320,128]{2,1,0:T(8,128)(2,1)}, u32[]{:S(2)}) copy-start(bf16[3,320,128]{2,1,0:T(8,128)(2,1)} %constant.28.clone.sel) | copy-start | bytes 737284
  56.0 1.1 %copy-start = (bf16[64,40,128]{2,1,0:T(8,128)(2,1)S(1)}, bf16[64,40,128]{2,1,0:T(8,128)(2,1)}, u32[]{:S(2)}) copy-start(bf16[64,40,128]{2,1,0:T(8,128)(2,1)} %shard_map.199.recv) | copy-start | bytes 1966084

commit v2 on v1

--- a/solution.py
+++ b/solution.py
@@ -128,12 +128,13 @@
     tokens, mask, w_qkv, w_proj, w_up, w_down, query, w_dec_q, w_dec_kv, w_dec_o, decode_t,
     c_pick, c_pick2, c_level, c_out, c_mrow, c_mcol, c_seam, c_order,
     recv,
-    tok, own, hsend, hrecv, xone, b_qkv, b_proj, b_up, b_down, b_kg, b_dq, qbd,
+    tok, own, hsend, hrecv, xone, normed, b_qkv, b_proj, b_up, b_down, b_kg, b_dq, qbd,
     v_query, v_dq, v_dkv, v_do, v_dec, pick, pick2, level, outm, mrow, mcol, seam, order,
     mask_own, mask_right, marks, hidden, diff, dwt, zpix, msg,
     lsem, wsend, wrecv, hssem, hrsem, osend, orecv, heard,
 ):
     dests, band, rows = sizes(grid)
+    assert grid & (grid - 1) == 0
     me = lax.axis_index("grid")
     v = lax.axis_index("var")
     partner = {"var": 1 - v}
@@ -227,8 +228,10 @@
     for i in range(3):
         local[i].wait()
     pack(0, hsend)
-    for step in range(SLOTS):
+    def send_halo(step):
         halo(lax.rem(me + grid - 1 + step, SLOTS)).start()
+
+    send_halo(0)
     local[3].wait()
     pack(18, own)
 
@@ -252,6 +255,7 @@
 
     for copy in shared[4:]:
         copy.start()
+    send_halo(1)
     hear(0)
     tell(1)
     zpix[...] = jnp.zeros_like(zpix)
@@ -276,6 +280,14 @@
         bias = jnp.where(diagonal, 0.0, bias)
         yield
         contexts = []
+
+        def head(scores, vs):
+            top = jnp.max(scores, axis=-1, keepdims=True)
+            probs = jnp.exp2((scores - top) * LOG2E).astype(BF)
+            both = dot(probs, jnp.concatenate([vs, ones], axis=1))
+            contexts.append(both[:, :128] * (1.0 / both[:, 128:]))
+
+        waiting = None
         for g in range(2):
             q = (dot(n1, b_qkv[g, 0]).astype(BF)) * BF(HD ** -0.5)
             k = dot(n1, b_qkv[g, 1]).astype(BF)
@@ -283,34 +295,32 @@
             yield
             for pair in range(2):
                 cut = slice(128 * pair, 128 * pair + 128)
-                context = None
                 for side in range(2):
                     inside = (pair_lane >= 64 * side) & (pair_lane < 64 * side + 64)
                     qs = jnp.where(inside, q[:, cut], BF(0))
                     vs = jnp.where(inside, val[:, cut], BF(0))
                     scores = dot_t(qs, k[:, cut]) + bias
-                    top = jnp.max(scores, axis=-1, keepdims=True)
-                    probs = jnp.exp2((scores - top) * LOG2E).astype(BF)
-                    both = dot(probs, jnp.concatenate([vs, ones], axis=1))
-                    part = both[:, :128] * (1.0 / both[:, 128:])
-                    context = part if context is None else context + part
+                    if waiting is not None:
+                        head(*waiting)
+                    waiting = scores, vs
                     yield
-                contexts.append(context.astype(BF))
+        head(*waiting)
+        contexts = [(contexts[2 * i] + contexts[2 * i + 1]).astype(BF) for i in range(4)]
         attended = dot(jnp.concatenate(contexts[:2], axis=1), b_proj[0])
-        xone[w] = x + attended + dot(jnp.concatenate(contexts[2:], axis=1), b_proj[1])
+        x1 = x + attended + dot(jnp.concatenate(contexts[2:], axis=1), b_proj[1])
+        xone[w] = x1
+        normed[w] = norm(x1)
         yield
 
     def finish(w):
-        x1 = xone[w]
-        n2 = norm(x1)
-        yield
+        n2 = normed[w]
         for g in range(2):
             for c in range(2):
                 h = dot(n2, b_up[g, :, 512 * c : 512 * c + 512])
                 h = 0.5 * h * (1.0 + lax.erf(h * (2.0 ** -0.5)))
                 hidden[:, 1024 * g + 512 * c : 1024 * g + 512 * c + 512] = h.astype(BF)
                 yield
-        grown = x1 + dot(hidden[:, :1024], b_down[0]) + dot(hidden[:, 1024:], b_down[1])
+        grown = xone[w] + dot(hidden[:, :1024], b_down[0]) + dot(hidden[:, 1024:], b_down[1])
         yield
         n3 = norm(grown.astype(BF).astype(F32))
         yield
@@ -336,15 +346,18 @@
                 diff[g, h, 1] = d1[64 * h : 64 * h + 64]
                 base = base + last_level[64 * h : 64 * h + 64]
         yield
-        for l in range(NLEV):
-            total = base
+        for group in ((0, 1, 2, 3), (4, 5, 6, 7), (8, 9, 10, 11, 12)):
+            totals = [base] * len(group)
             for g in range(2):
                 for h in range(4):
                     for j in range(2):
-                        total = total + dwt[g, j, 16 * h + l : 16 * h + l + 1, :] * diff[g, h, j]
-            zpix[pl.ds(l, 64, stride=16), :] = total
-            if l % 4 == 3:
-                yield
+                        step = diff[g, h, j]
+                        totals = [
+                            total + dwt[g, j, 16 * h + l : 16 * h + l + 1, :] * step for total, l in zip(totals, group)
+                        ]
+            for total, l in zip(totals, group):
+                zpix[pl.ds(l, 64, stride=16), :] = total
+            yield
         packed = jnp.zeros((dests * rows, 256), F32)
         for a in range(4):
             packed = packed + dot_t(outm[a], zpix[256 * a : 256 * a + 256, :].astype(BF))
@@ -353,34 +366,44 @@
                 msg[w, side, d] = packed[rows * d : rows * d + rows, 128 * side : 128 * side + 128].astype(BF)
         yield
 
-    def run(*parts):
-        parts = list(parts)
-        while parts:
-            parts = [part for part in parts if next(part, 0) is None]
+    def run(*parts, order=""):
+        for which in order:
+            next(parts[int(which)], None)
+        for part in parts:
+            for _ in part:
+                pass
+
+    my_window = lax.rem(me + grid - dests // 2, grid) // dests
 
     def send(w):
+        base = window_of(v, w) * dests + dests // 2
+        stays = window_of(v, w) == my_window
+
+        def one(d, side, to):
+            return remote(msg.at[w, side, d], recv.at[me], osend.at[w], orecv, {"grid": to, "var": side})
+
         for d in range(dests):
-            to = lax.rem(window_of(v, w) * dests + dests // 2 + d, grid)
-            for side in range(2):
-                mine = (to == me) & (v == side)
-
-                @pl.when(mine)
-                def _():
-                    pltpu.make_async_copy(msg.at[w, side, d], recv.at[me], orecv).start()
-
-                @pl.when(jnp.logical_not(mine))
-                def _():
-                    remote(msg.at[w, side, d], recv.at[me], osend.at[w], orecv, {"grid": to, "var": side}).start()
+            to = (base + d) & (grid - 1)
+            one(d, 1 - v, to).start()
+
+            @pl.when(jnp.logical_not(stays & (to == me)))
+            def _():
+                one(d, v, to).start()
+
+        @pl.when(stays)
+        def _():
+            d = (me - base) & (grid - 1)
+            pltpu.make_async_copy(msg.at[w, v, d], recv.at[me], orecv).start()
 
     first = lax.rem(me, SLOTS)
     halo(first).wait_recv()
-    hear(1)
-    tell(2)
+    send_halo(2)
+    send_halo(3)
     shared[0].wait()
     shared[1].wait()
     run(attend(first))
-    hear(2)
-    tell(3)
+    hear(1)
+    tell(2)
     for copy in shared[2:]:
         copy.wait()
     lane2 = lax.broadcasted_iota(jnp.int32, (16, 256), 1)
@@ -396,10 +419,12 @@
     def body(step, _):
         now, later = lax.rem(me + step, SLOTS), lax.rem(me + step + 1, SLOTS)
         halo(later).wait_recv()
-        run(finish(now), attend(later))
+        run(finish(now), attend(later), order="10000010110101101101101")
 
         @pl.when(step == 0)
         def _():
+            hear(2)
+            tell(3)
             hear(3)
 
         send(now)
@@ -409,8 +434,6 @@
     last = lax.rem(me + SLOTS - 1, SLOTS)
     run(finish(last))
     send(last)
-
-    my_window = lax.rem(me + grid - dests // 2, grid) // dests
 
     def sent(w, _):
         halo(w).wait_send()
@@ -492,15 +515,16 @@
     vm = pltpu.VMEM
     return pl.pallas_call(
         functools.partial(main_kernel, grid),
-        out_shape=jax.ShapeDtypeStruct((grid, rows, 128), BF),
+        out_shape=pltpu.VMEM((grid, rows, 128), BF),
         in_specs=[pl.BlockSpec(memory_space=pltpu.HBM)] * len(operands),
-        out_specs=pl.BlockSpec(memory_space=pl.ANY),
+        out_specs=pl.BlockSpec(memory_space=pltpu.VMEM),
         scratch_shapes=[
             vm((36, 48, 512), BF),
             vm((SLOTS, HALF, 512), BF),
             vm((SLOTS, HALF, 512), BF),
             vm((SLOTS, HALF, 512), BF),
             vm((SLOTS, TOK, 512), F32),
+            vm((SLOTS, TOK, 512), BF),
             vm((2, 3, 512, 256), BF),
             vm((2, 256, 512), BF),
             vm((2, 512, 1024), BF),
@@ -542,6 +566,7 @@
     tables = final_tables(grid)
     lines = pl.pallas_call(
         functools.partial(final_kernel, grid),
+        in_specs=[pl.BlockSpec(memory_space=pltpu.VMEM)] * 3,
         out_shape=jax.ShapeDtypeStruct((NLEV * band, 2, 48 * grid), F32),
         scratch_shapes=[pltpu.VMEM((band, 12 * grid, 128), F32)],
         compiler_params=pltpu.CompilerParams(vmem_limit_bytes=32 * 2**20),

time: 59.3 us -> 53.8 us (0.907)
  the two profiles are of different devices: /device:TPU:529 before, /device:TPU:513 now
where the time goes in v2:
time: 53.8 us; the launch traced here: 53.7 us
  Pallas kernels  53.6 us (100%)
    pallas_call x1, Pallas kernels, pixels_of(): pl.pallas_call(functools.partial(main_kernel, grid), out_shape=pltpu.VMEM...  51.6 us
    pallas_call x1, Pallas kernels, assemble(): pl.pallas_call(functools.partial(final_kernel, grid), in_specs=[pl.BlockS...  2.08 us

profile of v2, /device:TPU:513, one launch (start us, length us, event | category | flops | bytes accessed | tf_op | source)
XLA Modules:
  0.0 53.7 jit_solution(12885205923843903398)
XLA Ops:
  0.0 0.0 copy-start
  0.0 0.0 copy-start.1
  0.0 51.6 %shard_map.199.recv = bf16[64,40,128]{2,1,0:T(8,128)(2,1)S(1)} custom-call(bf16[36,48,512]{2,1,0:T(8,128)(2,1)} %bitcast.8, s32[12,48]{1,0:T(8,128)} %bitcast.10, bf16[3,512,256]{2,1,0:T(8,128)(2,1)} %w_qkv.1, bf16[256,512]{1,0:T(8,128)(2,1)} %w_proj.1, bf16[512,1024]{1,0:T(8,128)(2,1)} %w_up.1, bf16[1024,512]{1,0:T(8,128)(2,1)} %w_down.1, ...), custom_call_target="tpu_custom_call" | custom-call | tf_op jit(solution)/shard_map/pallas_call | solution.py:516
  51.6 0.0 copy-done
  51.6 0.0 copy-done.1
  51.6 2.1 %shard_map.200 = f32[39,2,3072]{2,1,0:T(2,128)} custom-call(bf16[64,40,128]{2,1,0:T(8,128)(2,1)S(1)} %shard_map.199.recv, bf16[3,320,128]{2,1,0:T(8,128)(2,1)S(1)} %copy-done.1, bf16[2,256,512]{2,1,0:T(8,128)(2,1)S(1)} %copy-done), custom_call_target="tpu_custom_call" | custom-call | tf_op jit(solution)/shard_map/pallas_call | solution.py:567
Async XLA Ops:
  0.0 51.6 %copy-start = (bf16[2,256,512]{2,1,0:T(8,128)(2,1)S(1)}, bf16[2,256,512]{2,1,0:T(8,128)(2,1)}, u32[]{:S(2)}) copy-start(bf16[2,256,512]{2,1,0:T(8,128)(2,1)} %constant.29.clone.spread) | copy-start | bytes 1572868
  0.0 51.6 %copy-start.1 = (bf16[3,320,128]{2,1,0:T(8,128)(2,1)S(1)}, bf16[3,320,128]{2,1,0:T(8,128)(2,1)}, u32[]{:S(2)}) copy-start(bf16[3,320,128]{2,1,0:T(8,128)(2,1)} %constant.28.clone.sel) | copy-start | bytes 737284

commit v3 on v2

--- a/solution.py
+++ b/solution.py
@@ -219,19 +219,23 @@
         for w in range(SLOTS):
             target[w, 96:112, :] = packed[16 * w : 16 * w + 16]
 
-    pl.semaphore_wait(barrier, 5)
-    for copy in shared[:4]:
-        copy.start()
-    mask_copy.start()
-    tell(0)
+    def send_halo(step):
+        halo(lax.rem(me + grid - 1 + step, SLOTS)).start()
 
     for i in range(3):
         local[i].wait()
     pack(0, hsend)
-    def send_halo(step):
-        halo(lax.rem(me + grid - 1 + step, SLOTS)).start()
-
+    pl.semaphore_wait(barrier, 5)
+    tell(0)
+    mask_copy.start()
     send_halo(0)
+    shared[0].start()
+    shared[1].start()
+    send_halo(1)
+    shared[2].start()
+    send_halo(2)
+    shared[3].start()
+    send_halo(3)
     local[3].wait()
     pack(18, own)
 
@@ -255,7 +259,6 @@
 
     for copy in shared[4:]:
         copy.start()
-    send_halo(1)
     hear(0)
     tell(1)
     zpix[...] = jnp.zeros_like(zpix)
@@ -397,8 +400,6 @@
 
     first = lax.rem(me, SLOTS)
     halo(first).wait_recv()
-    send_halo(2)
-    send_halo(3)
     shared[0].wait()
     shared[1].wait()
     run(attend(first))

time: 53.8 us -> 53.3 us (level)
  no operation moved by 1% of the time
where the time goes in v3:
time: 53.3 us
  Pallas kernels  53.2 us (100%)
    pallas_call x1, Pallas kernels, pixels_of(): pl.pallas_call(functools.partial(main_kernel, grid), out_shape=pltpu.VMEM...  51.1 us
    pallas_call x1, Pallas kernels, assemble(): pl.pallas_call(functools.partial(final_kernel, grid), in_specs=[pl.BlockS...  2.08 us

profile of v3, /device:TPU:513, one launch (start us, length us, event | category | flops | bytes accessed | tf_op | source)
XLA Modules:
  0.0 53.3 jit_solution(16313434839536825738)
XLA Ops:
  0.0 0.0 copy-start
  0.0 0.0 copy-start.1
  0.0 51.1 %shard_map.199.recv = bf16[64,40,128]{2,1,0:T(8,128)(2,1)S(1)} custom-call(bf16[36,48,512]{2,1,0:T(8,128)(2,1)} %bitcast.8, s32[12,48]{1,0:T(8,128)} %bitcast.10, bf16[3,512,256]{2,1,0:T(8,128)(2,1)} %w_qkv.1, bf16[256,512]{1,0:T(8,128)(2,1)} %w_proj.1, bf16[512,1024]{1,0:T(8,128)(2,1)} %w_up.1, bf16[1024,512]{1,0:T(8,128)(2,1)} %w_down.1, ...), custom_call_target="tpu_custom_call" | custom-call | tf_op jit(solution)/shard_map/pallas_call | solution.py:517
  51.2 0.0 copy-done
  51.2 0.0 copy-done.1
  51.2 2.1 %shard_map.200 = f32[39,2,3072]{2,1,0:T(2,128)} custom-call(bf16[64,40,128]{2,1,0:T(8,128)(2,1)S(1)} %shard_map.199.recv, bf16[3,320,128]{2,1,0:T(8,128)(2,1)S(1)} %copy-done.1, bf16[2,256,512]{2,1,0:T(8,128)(2,1)S(1)} %copy-done), custom_call_target="tpu_custom_call" | custom-call | tf_op jit(solution)/shard_map/pallas_call | solution.py:568
Async XLA Ops:
  0.0 51.2 %copy-start = (bf16[2,256,512]{2,1,0:T(8,128)(2,1)S(1)}, bf16[2,256,512]{2,1,0:T(8,128)(2,1)}, u32[]{:S(2)}) copy-start(bf16[2,256,512]{2,1,0:T(8,128)(2,1)} %constant.29.clone.spread) | copy-start | bytes 1572868
  0.0 51.2 %copy-start.1 = (bf16[3,320,128]{2,1,0:T(8,128)(2,1)S(1)}, bf16[3,320,128]{2,1,0:T(8,128)(2,1)}, u32[]{:S(2)}) copy-start(bf16[3,320,128]{2,1,0:T(8,128)(2,1)} %constant.28.clone.sel) | copy-start | bytes 737284

commit v4 on v3

--- a/solution.py
+++ b/solution.py
@@ -42,8 +42,8 @@
     for k in range(grid):
         ways = [abs(b) + min((k - stride * b) % grid, (stride * b - k) % grid) for b in range(-stride, stride + 1)]
         radius = max(radius, min(ways))
-    rounds = max(0, (radius - 1).bit_length())
-    assert rounds <= 3
+    rounds = max(0, (radius - 1).bit_length() - 1)
+    assert rounds <= 2
     return stride, rounds
 
 
@@ -148,13 +148,16 @@
     stride, rounds = reach(grid)
     sides = (1, grid - 1, stride, grid - stride)
     signal(barrier, partner)
-    for by in sides:
+    near = sides + tuple(
+        (a + b) % grid for a, b in ((2, 0), (-2, 0), (0, 2 * stride), (0, -2 * stride)) + tuple((x, y * stride) for x in (1, -1) for y in (1, -1))
+    )
+    for by in near:
         signal(barrier, {"grid": lax.rem(me + by, grid)})
 
     def tell(k):
         if k < rounds:
             for by in sides:
-                signal(heard.at[k], {"grid": lax.rem(me + by * 2**k, grid)})
+                signal(heard.at[k], {"grid": lax.rem(me + by * 2 ** (k + 1), grid)})
         elif k == rounds:
             signal(heard.at[k], partner)
 
@@ -225,7 +228,7 @@
     for i in range(3):
         local[i].wait()
     pack(0, hsend)
-    pl.semaphore_wait(barrier, 5)
+    pl.semaphore_wait(barrier, 1 + len(near))
     tell(0)
     mask_copy.start()
     send_halo(0)
@@ -320,10 +323,10 @@
         for g in range(2):
             for c in range(2):
                 h = dot(n2, b_up[g, :, 512 * c : 512 * c + 512])
-                h = 0.5 * h * (1.0 + lax.erf(h * (2.0 ** -0.5)))
+                h = h * (1.0 + lax.erf(h * (2.0 ** -0.5)))
                 hidden[:, 1024 * g + 512 * c : 1024 * g + 512 * c + 512] = h.astype(BF)
                 yield
-        grown = xone[w] + dot(hidden[:, :1024], b_down[0]) + dot(hidden[:, 1024:], b_down[1])
+        grown = xone[w] + 0.5 * (dot(hidden[:, :1024], b_down[0]) + dot(hidden[:, 1024:], b_down[1]))
         yield
         n3 = norm(grown.astype(BF).astype(F32))
         yield
@@ -385,18 +388,25 @@
         def one(d, side, to):
             return remote(msg.at[w, side, d], recv.at[me], osend.at[w], orecv, {"grid": to, "var": side})
 
-        for d in range(dests):
-            to = (base + d) & (grid - 1)
-            one(d, 1 - v, to).start()
-
-            @pl.when(jnp.logical_not(stays & (to == me)))
-            def _():
-                one(d, v, to).start()
+        @pl.when(jnp.logical_not(stays))
+        def _():
+            for d in range(dests):
+                for side in range(2):
+                    one(d, side, (base + d) & (grid - 1)).start()
 
         @pl.when(stays)
         def _():
-            d = (me - base) & (grid - 1)
-            pltpu.make_async_copy(msg.at[w, v, d], recv.at[me], orecv).start()
+            own_band = (me - base) & (grid - 1)
+
+            def away(k, _):
+                d = (own_band + k) & (dests - 1)
+                for side in range(2):
+                    one(d, side, (base + d) & (grid - 1)).start()
+                return 0
+
+            lax.fori_loop(1, dests, away, 0)
+            one(own_band, 1 - v, me).start()
+            pltpu.make_async_copy(msg.at[w, v, own_band], recv.at[me], orecv).start()
 
     first = lax.rem(me, SLOTS)
     halo(first).wait_recv()
@@ -487,8 +497,11 @@
                 stage[slot, start : start + 6, :] = piece[:6]
                 stage[slot, 0:6, :] = piece[6:]
     flipped = jnp.zeros((4 * pad, cells), F32)
-    for slot in range(band):
-        flipped = flipped + dot_t(sel[slot], stage[slot].astype(BF))
+    for slot in range(0, band, 2):
+        group = range(slot, min(slot + 2, band))
+        picks = jnp.concatenate([sel[k] for k in group], axis=1)
+        cells_of = jnp.concatenate([stage[k].astype(BF) for k in group], axis=1)
+        flipped = flipped + dot_t(picks, cells_of)
     flipped = flipped.astype(BF)
     tile = spread.shape[2] // 4
     tiles = cells // tile

time: 53.3 us -> 52.1 us (0.977)
  Pallas kernels: 53.2 us -> 52 us
    pallas_call x1, Pallas kernels: 51.1 us -> 50.1 us  [pixels_of(): pl.pallas_call(functools.partial(main_kernel, grid), out_shape=pltpu.VMEM...]
where the time goes in v4:
time: 52.1 us; the launch traced here: 52 us
  Pallas kernels  52 us (100%)
    pallas_call x1, Pallas kernels, pixels_of(): pl.pallas_call(functools.partial(main_kernel, grid), out_shape=pltpu.VMEM...  50.1 us
    pallas_call x1, Pallas kernels, assemble(): pl.pallas_call(functools.partial(final_kernel, grid), in_specs=[pl.BlockS...  1.87 us

profile of v4, /device:TPU:513, one launch (start us, length us, event | category | flops | bytes accessed | tf_op | source)
XLA Modules:
  0.0 52.0 jit_solution(16377378668667193832)
XLA Ops:
  0.0 0.0 copy-start
  0.0 0.0 copy-start.1
  0.0 50.1 %shard_map.199.recv = bf16[64,40,128]{2,1,0:T(8,128)(2,1)S(1)} custom-call(bf16[36,48,512]{2,1,0:T(8,128)(2,1)} %bitcast.8, s32[12,48]{1,0:T(8,128)} %bitcast.10, bf16[3,512,256]{2,1,0:T(8,128)(2,1)} %w_qkv.1, bf16[256,512]{1,0:T(8,128)(2,1)} %w_proj.1, bf16[512,1024]{1,0:T(8,128)(2,1)} %w_up.1, bf16[1024,512]{1,0:T(8,128)(2,1)} %w_down.1, ...), custom_call_target="tpu_custom_call" | custom-call | tf_op jit(solution)/shard_map/pallas_call | solution.py:530
  50.1 0.0 copy-done
  50.1 0.0 copy-done.1
  50.1 1.9 %shard_map.200 = f32[39,2,3072]{2,1,0:T(2,128)} custom-call(bf16[64,40,128]{2,1,0:T(8,128)(2,1)S(1)} %shard_map.199.recv, bf16[3,320,128]{2,1,0:T(8,128)(2,1)S(1)} %copy-done.1, bf16[2,256,512]{2,1,0:T(8,128)(2,1)S(1)} %copy-done), custom_call_target="tpu_custom_call" | custom-call | tf_op jit(solution)/shard_map/pallas_call | solution.py:581
Async XLA Ops:
  0.0 50.1 %copy-start = (bf16[2,256,512]{2,1,0:T(8,128)(2,1)S(1)}, bf16[2,256,512]{2,1,0:T(8,128)(2,1)}, u32[]{:S(2)}) copy-start(bf16[2,256,512]{2,1,0:T(8,128)(2,1)} %constant.29.clone.spread) | copy-start | bytes 1572868
  0.0 50.1 %copy-start.1 = (bf16[3,320,128]{2,1,0:T(8,128)(2,1)S(1)}, bf16[3,320,128]{2,1,0:T(8,128)(2,1)}, u32[]{:S(2)}) copy-start(bf16[3,320,128]{2,1,0:T(8,128)(2,1)} %constant.28.clone.sel) | copy-start | bytes 737284

commit v5 on v4

--- a/solution.py
+++ b/solution.py
@@ -32,8 +32,11 @@
 def sizes(grid):
     dests = grid // 8
     band = WIN * PIX // dests
-    rows = -(-(band * 12) // 8) * 8
-    return dests, band, rows
+    return dests, band, band * 12
+
+
+def pitch_of(rows):
+    return -(-rows // 8) * 8
 
 
 def reach(grid):
@@ -72,12 +75,13 @@
     t = np.arange(TOK)[valid]
     patch = half * 36 + c6 * 6 + r
     level_rows[j[valid] * 128 + patch[valid], t] = 1
-    out_rows = np.zeros((4, dests * rows, 128), np.float32)
+    pitch = pitch_of(rows)
+    out_rows = np.zeros((4, dests * pitch, 128), np.float32)
     for d in range(dests):
         for slot in range(band):
             rr, a = divmod(band * d + slot, 4)
             for c in range(12):
-                out_rows[a, d * rows + slot * 12 + c, (c // 6) * 36 + (c % 6) * 6 + rr] = 1
+                out_rows[a, d * pitch + slot * 12 + c, (c // 6) * 36 + (c % 6) * 6 + rr] = 1
     mask_rows = np.zeros((8, 48, TOK), np.float32)
     for window in range(8):
         mask_rows[window, ((6 * window + 3 + r) % 48)[valid], t] = 1
@@ -230,8 +234,8 @@
     pack(0, hsend)
     pl.semaphore_wait(barrier, 1 + len(near))
     tell(0)
+    send_halo(0)
     mask_copy.start()
-    send_halo(0)
     shared[0].start()
     shared[1].start()
     send_halo(1)
@@ -364,12 +368,13 @@
             for total, l in zip(totals, group):
                 zpix[pl.ds(l, 64, stride=16), :] = total
             yield
-        packed = jnp.zeros((dests * rows, 256), F32)
+        pitch = pitch_of(rows)
+        packed = jnp.zeros((dests * pitch, 256), F32)
         for a in range(4):
             packed = packed + dot_t(outm[a], zpix[256 * a : 256 * a + 256, :].astype(BF))
         for d in range(dests):
             for side in range(2):
-                msg[w, side, d] = packed[rows * d : rows * d + rows, 128 * side : 128 * side + 128].astype(BF)
+                msg[w, side, d] = packed[pitch * d : pitch * d + rows, 128 * side : 128 * side + 128].astype(BF)
         yield
 
     def run(*parts, order=""):

time: 52.1 us -> 52.1 us (level)
  no operation moved by 1% of the time
where the time goes in v5:
time: 52.1 us; the launch traced here: 52 us
  Pallas kernels  52 us (100%)
    pallas_call x1, Pallas kernels, pixels_of(): pl.pallas_call(functools.partial(main_kernel, grid), out_shape=pltpu.VMEM...  50.1 us
    pallas_call x1, Pallas kernels, assemble(): pl.pallas_call(functools.partial(final_kernel, grid), in_specs=[pl.BlockS...  1.86 us

profile of v5, /device:TPU:513, one launch (start us, length us, event | category | flops | bytes accessed | tf_op | source)
XLA Modules:
  0.0 52.0 jit_solution(4983769565063158664)
XLA Ops:
  0.0 0.0 copy-start
  0.0 0.0 copy-start.1
  0.0 50.1 %shard_map.199.recv = bf16[64,36,128]{2,1,0:T(8,128)(2,1)S(1)} custom-call(bf16[36,48,512]{2,1,0:T(8,128)(2,1)} %bitcast.8, s32[12,48]{1,0:T(8,128)} %bitcast.10, bf16[3,512,256]{2,1,0:T(8,128)(2,1)} %w_qkv.1, bf16[256,512]{1,0:T(8,128)(2,1)} %w_proj.1, bf16[512,1024]{1,0:T(8,128)(2,1)} %w_up.1, bf16[1024,512]{1,0:T(8,128)(2,1)} %w_down.1, ...), custom_call_target="tpu_custom_call" | custom-call | tf_op jit(solution)/shard_map/pallas_call | solution.py:535
  50.1 0.0 copy-done
  50.1 0.0 copy-done.1
  50.1 1.9 %shard_map.200 = f32[39,2,3072]{2,1,0:T(2,128)} custom-call(bf16[64,36,128]{2,1,0:T(8,128)(2,1)S(1)} %shard_map.199.recv, bf16[3,320,128]{2,1,0:T(8,128)(2,1)S(1)} %copy-done.1, bf16[2,256,512]{2,1,0:T(8,128)(2,1)S(1)} %copy-done), custom_call_target="tpu_custom_call" | custom-call | tf_op jit(solution)/shard_map/pallas_call | solution.py:586
Async XLA Ops:
  0.0 50.1 %copy-start = (bf16[2,256,512]{2,1,0:T(8,128)(2,1)S(1)}, bf16[2,256,512]{2,1,0:T(8,128)(2,1)}, u32[]{:S(2)}) copy-start(bf16[2,256,512]{2,1,0:T(8,128)(2,1)} %constant.29.clone.spread) | copy-start | bytes 1572868
  0.0 50.1 %copy-start.1 = (bf16[3,320,128]{2,1,0:T(8,128)(2,1)S(1)}, bf16[3,320,128]{2,1,0:T(8,128)(2,1)}, u32[]{:S(2)}) copy-start(bf16[3,320,128]{2,1,0:T(8,128)(2,1)} %constant.28.clone.sel) | copy-start | bytes 737284
